TPU v7x, 32 devices: a whole 2x2x4 slice. The times are simulated.
32 devices in a mesh: group: 2 (over x), expert: 16 (over z, y, core).
Axes of the slice: x: 2, y: 2, z: 4, core: 2. Of those that a mesh axis runs over, the one named last changes fastest.
Arguments:
- query: bfloat16 [32, 2048], P(('group', 'expert')), parts along dimension 0, may hold values from -600 to 600
- key_new: bfloat16 [32, 2048], P(('group', 'expert')), parts along dimension 0, may hold values from -6 to 6
- value_new: bfloat16 [32, 2048], P(('group', 'expert')), parts along dimension 0, may hold values from -6 to 6
- key_cache: bfloat16 [32, 256, 2048], P(('group', 'expert')), parts along dimension 0, may hold values from -6 to 6
- value_cache: bfloat16 [32, 256, 2048], P(('group', 'expert')), parts along dimension 0, may hold values from -6 to 6
- lengths: int32 [32], P(('group', 'expert')), parts along dimension 0, may hold values from 1 to 256
- hidden: bfloat16 [32, 2048], P(('group', 'expert')), parts along dimension 0, may hold values from -6 to 6
- routes: int32 [32], P('group'), parts along dimension 0, may hold values from 0 to 31, as said below
- w_out: bfloat16 [2048, 2048], P(None, 'expert'), may hold values from -0.125 to 0.125
- ln_gain: bfloat16 [2048], replicated, may hold values from 0.099609375 to 1.8984375
- router: bfloat16 [2048, 32], replicated, may hold values from -0.125 to 0.125
- shared_up: bfloat16 [2048, 8192], P(None, 'expert'), may hold values from -0.125 to 0.125
- shared_down: bfloat16 [8192, 2048], P('expert'), may hold values from -0.0625 to 0.0625
- expert_up: bfloat16 [2048, 131072], P(None, 'expert'), may hold values from -0.125 to 0.125
- expert_down: bfloat16 [131072, 2048], P('expert'), may hold values from -0.09375 to 0.09375
Outputs:
- layer_out: bfloat16 [32, 2048], P(('group', 'expert')), parts along dimension 0
There are 2 independent parts, one for each index of `group`. A program takes and returns all parts, laid end to end along the dimension named above; an argument that names none is the same for every part. Nothing has to cross between parts.
Inputs may be any that keep to these rules, and one draw needn't show every extreme that they name: `routes`: no expert is named by more than 2 tokens of the group, and in every draw some expert is named by exactly 2.
All inputs are finite; a program needn't handle non-finite values.
Results may differ from a plain program's by a relative error of at most 0.0085.
Values may be sent and summed in bfloat16 or wider, within the bound.
No kernel may reach another device: no remote copies, remote signals or barrier semaphores. Data moves between devices by JAX's collectives and lax.ppermute only.
A program may use at most 128 MiB of HBM per device.

v0:
```python
import math
import jax
import jax.numpy as jnp
from jax import lax
from jax.sharding import PartitionSpec as P

D = 2048
HEADS = 16
HEAD_DIM = 128
FF = 4096
EXPERTS = 32


def attend(query, key_new, value_new, key_cache, value_cache, lengths):
    seq_count = query.shape[0]
    cache_len = key_cache.shape[1]
    scale_factor = 1.0 / math.sqrt(HEAD_DIM)
    head_query = query.reshape(seq_count, HEADS, HEAD_DIM)
    head_keys = key_cache.reshape(seq_count, cache_len, HEADS, HEAD_DIM)
    head_values = value_cache.reshape(seq_count, cache_len, HEADS, HEAD_DIM)
    scores = (
        jnp.einsum("shd,schd->shc", head_query, head_keys, preferred_element_type=jnp.float32)
        * scale_factor
    )
    own_score = (
        jnp.einsum(
            "shd,shd->sh",
            head_query,
            key_new.reshape(seq_count, HEADS, HEAD_DIM),
            preferred_element_type=jnp.float32,
        )
        * scale_factor
    )
    positions = jnp.arange(cache_len, dtype=jnp.int32)
    scores = jnp.where(positions[None, None, :] < lengths[:, None, None], scores, -1e30)
    top_score = jnp.maximum(jnp.max(scores, axis=2), own_score)
    weights = jnp.exp(scores - top_score[:, :, None])
    own_weight = jnp.exp(own_score - top_score)
    normalizer = jnp.sum(weights, axis=2) + own_weight
    weights = (weights / normalizer[:, :, None]).astype(jnp.bfloat16)
    own_weight = (own_weight / normalizer).astype(jnp.bfloat16)
    mixed_values = jnp.einsum(
        "shc,schd->shd", weights, head_values, preferred_element_type=jnp.float32
    )
    mixed_values = mixed_values + own_weight.astype(jnp.float32)[:, :, None] * value_new.reshape(
        seq_count, HEADS, HEAD_DIM
    ).astype(jnp.float32)
    return mixed_values.reshape(seq_count, HEADS * HEAD_DIM).astype(jnp.bfloat16)


def body(
    query,
    key_new,
    value_new,
    key_cache,
    value_cache,
    lengths,
    hidden,
    routes,
    w_out,
    ln_gain,
    router,
    shared_up,
    shared_down,
    expert_up,
    expert_down,
):
    seq_count = query.shape[0]
    attended = attend(query, key_new, value_new, key_cache, value_cache, lengths)
    every_attended, every_hidden = (
        lax.all_gather(attended, "expert", axis=0, tiled=True),
        lax.all_gather(hidden, "expert", axis=0, tiled=True),
    )
    projected = jnp.dot(every_attended, w_out, preferred_element_type=jnp.float32).astype(
        jnp.bfloat16
    )
    every_projected = lax.all_gather(projected, "expert", axis=1, tiled=True)
    residual = every_hidden.astype(jnp.float32) + every_projected.astype(jnp.float32)
    centered = residual - jnp.mean(residual, axis=1, keepdims=True)
    variance = jnp.mean(centered * centered, axis=1, keepdims=True)
    normed = (
        centered / jnp.sqrt(jnp.maximum(variance, 0.25)) * ln_gain.astype(jnp.float32)
    ).astype(jnp.bfloat16)
    logits = jnp.dot(normed, router, preferred_element_type=jnp.float32)
    all_experts = jnp.arange(EXPERTS, dtype=jnp.int32)
    chosen = jnp.sum(jnp.where(routes[:, None] == all_experts[None, :], logits, 0.0), axis=1)
    gate_value = jax.nn.sigmoid(chosen)
    shared_hidden = jax.nn.gelu(
        jnp.dot(normed, shared_up, preferred_element_type=jnp.float32), approximate=True
    ).astype(jnp.bfloat16)
    total_tokens = routes.shape[0]
    capacity = 4 * total_tokens // EXPERTS
    column_count = expert_up.shape[1]
    local_units = min(column_count, FF)
    local_experts = column_count // local_units
    device_index = lax.axis_index("expert")
    first_expert = device_index * column_count // FF
    expert_ids = first_expert + jnp.arange(local_experts, dtype=jnp.int32)
    member = routes[:, None] == expert_ids[None, :]
    slot_rank = jnp.cumsum(member.astype(jnp.int32), axis=0) - 1
    slot_ids = jnp.arange(capacity, dtype=jnp.int32)
    placed = member[:, :, None] & (slot_rank[:, :, None] == slot_ids[None, None, :])
    picked = jnp.einsum(
        "skc,sd->kcd", placed.astype(jnp.bfloat16), normed, preferred_element_type=jnp.float32
    ).astype(jnp.bfloat16)
    up_local = expert_up.reshape(D, local_experts, local_units)
    inner_act = jax.nn.gelu(
        jnp.einsum("kcd,dkf->kcf", picked, up_local, preferred_element_type=jnp.float32),
        approximate=True,
    ).astype(jnp.bfloat16)
    down_local = expert_down.reshape(local_experts, local_units, D)
    result = jnp.einsum("kcf,kfd->kcd", inner_act, down_local, preferred_element_type=jnp.float32)
    spread = placed.astype(jnp.float32) * gate_value[:, None, None]
    summed = lax.psum_scatter(
        jnp.dot(shared_hidden, shared_down, preferred_element_type=jnp.float32)
        + jnp.einsum("skc,kcd->sd", spread, result, precision=lax.Precision.HIGHEST),
        "expert",
        scatter_dimension=0,
        tiled=True,
    )
    own_residual = lax.dynamic_slice_in_dim(residual, device_index * seq_count, seq_count, 0)
    combined = own_residual + summed
    return combined.astype(jnp.bfloat16)


def solution(mesh):
    placed = (
        P(("group", "expert"), None),
        P(("group", "expert"), None),
        P(("group", "expert"), None),
        P(("group", "expert"), None, None),
        P(("group", "expert"), None, None),
        P(("group", "expert")),
        P(("group", "expert"), None),
        P("group"),
        P(None, "expert"),
        P(),
        P(),
        P(None, "expert"),
        P("expert", None),
        P(None, "expert"),
        P("expert", None),
    )
    return jax.shard_map(
        body, mesh=mesh, in_specs=placed, out_specs=P(("group", "expert"), None), check_vma=False
    )
```

profile of v0, /device:TPU:8, one launch (start us, length us, event | category | flops | bytes accessed | tf_op | source)
XLA Modules:
  0.0 203.4 jit_solution(5360927554412156418)
XLA Ops:
  6.5 1.6 copy.43
  8.8 0.9 fusion.42
  9.8 0.7 reduce.5
  10.5 0.7 reduce.6
  11.5 0.2 fusion.38
  11.8 1.5 copy.47
  13.2 0.7 convert_element_type.86
  13.9 0.3 fusion.4
  14.4 19.2 %all-gather.1 = bf16[16,1,2048]{2,1,0:T(2,128)(2,1)S(1)} all-gather(bf16[1,1,2048]{2,1,0:T(2,128)(2,1)S(1)} %reshape.187), channel_id=1, replica_groups=mesh['group'=2,'expert'=16] {'expert'}, dimensions={0}, use_global_device_ids=true | all-gather | bytes 69632 | tf_op jit(solution)/shard_map/all_gather | solution.py:71
  33.5 1.2 convolution_convert_fusion.1
  34.8 17.6 %all_gather.11 = bf16[16,2048]{1,0:T(8,128)(2,1)S(1)} all-gather(bf16[16,128]{1,0:T(8,128)(2,1)S(1)} %convolution_convert_fusion.1), channel_id=1, replica_groups=mesh['group'=2,'expert'=16] {'expert'}, dimensions={1}, use_global_device_ids=true | all-gather | bytes 69632 | tf_op jit(solution)/shard_map/all_gather | solution.py:77
  52.4 19.3 %all-gather = bf16[16,1,2048]{2,1,0:T(2,128)(2,1)S(1)} all-gather(bf16[1,1,2048]{2,1,0:T(2,128)(2,1)} %bitcast.69), channel_id=1, replica_groups=mesh['group'=2,'expert'=16] {'expert'}, dimensions={0}, use_global_device_ids=true | all-gather | bytes 69632 | tf_op jit(solution)/shard_map/all_gather | solution.py:72
  71.7 0.2 fusion.57
  71.9 0.2 multiply_reduce_fusion
  72.1 0.7 convert_element_type.79
  72.8 0.7 fusion.56
  73.8 1.2 fusion.3
  75.0 12.2 %fusion.15 = bf16[2,2,4096]{2,1,0:T(2,128)(2,1)S(1)} fusion(bf16[256,2,8,4096]{3,2,1,0:T(8,128)(2,1)} %bitcast.63, bf16[16,2048]{1,0:T(8,128)(2,1)S(1)} %multiply_convert_fusion, pred[16,2,2]{0,1,2:T(4,128)(4,1)S(1)} %compare_and_fusion), kind=kOutput, calls=%fused_computation.22 | convolution fusion | flops 67526656 | bytes 33652800 | tf_op jit(solution)/shard_map/kcd,dkf->kcf/dot_general | solution.py:108
  87.3 12.8 %fusion.60 = f32[2,2,2048]{2,1,0:T(2,128)S(1)} fusion(bf16[2,2,4096]{2,1,0:T(2,128)(2,1)S(1)} %fusion.15, bf16[2,4096,2048]{2,1,0:T(8,128)(2,1)} %bitcast.64), kind=kOutput, calls=%fused_computation.80 | convolution fusion | flops 67108864 | bytes 33619968 | tf_op jit(solution)/shard_map/kcf,kfd->kcd/dot_general | solution.py:112
  100.1 0.4 convolution_bitcast_fusion
  100.5 3.0 %convolution_add_fusion = f32[16,2048]{1,0:T(8,128)} fusion(f32[16,2048]{1,0:T(8,128)S(1)} %convolution_bitcast_fusion, bf16[512,2048]{1,0:T(8,128)(2,1)S(1)} %copy-done, bf16[16,2048]{1,0:T(8,128)(2,1)S(1)} %multiply_convert_fusion, bf16[2048,512]{1,0:T(8,128)(2,1)} %param.26), kind=kOutput, calls=%fused_computation.4 | convolution fusion | flops 67215360 | bytes 4521984 | tf_op jit(solution)/shard_map/dot_general | solution.py:115
  103.5 0.6 dynamic-slice
  104.2 90.3 %all-reduce.3.cloned.1.call-done = f32[16,2048]{1,0:T(8,128)} async-done(((f32[16,2048]{1,0:T(8,128)}), f32[16,2048]{1,0:T(8,128)}) %all-reduce.3.cloned.1.call-update) | async-done | bytes 131088
  194.5 2.1 %fusion.40 = bf16[1,2048]{1,0:T(2,128)(2,1)} fusion(f32[16,2048]{1,0:T(8,128)} %all-reduce.3.cloned.1.call-done, u32[]{:T(128)} %bitcast.14, f32[16,2048]{1,0:T(8,128)S(1)} %get-tuple-element.6, s32[]{:T(128)S(6)} %select_n.18), kind=kLoop, calls=%fused_computation.48 | loop fusion | flops 4096 | bytes 20488 | tf_op jit(solution)/shard_map/convert_element_type | solution.py:123
  (24 shorter events, 0.8 us)
Async XLA Ops:
  6.5 93.9 %copy-start = (bf16[512,2048]{1,0:T(8,128)(2,1)S(1)}, bf16[512,2048]{1,0:T(8,128)(2,1)}, u32[]{:S(2)}) copy-start(bf16[512,2048]{1,0:T(8,128)(2,1)} %param.27) | copy-start | bytes 6291460
  6.5 187.9 %all-reduce.3.cloned.1.call-start = ((), (), s32[]{:S(2)}) async-start(), calls=%async_computation | async-start | bytes 262144
  87.2 16.3 %copy-start.1 = (u32[32]{0:T(128)S(1)}, u32[32]{0:T(128)}, u32[]{:S(2)}) copy-start(u32[32]{0:T(128)} %constant.69) | copy-start | bytes 388
Sparse Core Ops, SparseCore 0:
  103.6 90.8 all-reduce.2
where the time goes:
time: 204 us; the launch traced here: 203 us
  waiting for transfers between devices  90.3 us (44%)
  blocking collectives  56.1 us (28%)
  matrix products  32 us (16%)
  between operations  14.2 us (7%)
  other arithmetic  6.8 us (3%)
  local copies, waits for them, and re-layouts  3.92 us (2%)
    unnamed x2, waiting for transfers between devices  90.3 us
    all_gather x1, blocking collectives, body(): lax.all_gather(hidden, 'expert', axis=0, tiled=True)  19.3 us
    all_gather x1, blocking collectives, body(): lax.all_gather(attended, 'expert', axis=0, tiled=True)  19.2 us
    all_gather x1, blocking collectives, body(): every_projected = lax.all_gather(projected, 'expert', axis=1, tiled=True)  17.6 us
    dot_general x1, matrix products, body(): jnp.einsum('kcf,kfd->kcd', inner_act, down_local, preferred_element_type=...  12.8 us
    dot_general x1, matrix products, body(): jnp.einsum('kcd,dkf->kcf', picked, up_local, preferred_element_type=jnp.f...  12.2 us
  transfers between devices with their start and end apart: 1, of which 1 were waited for; matrix products, arithmetic and copies ran while one was open for 0% of the time, Pallas kernels for 0%

commit v1 on v0

--- a/solution.py
+++ b/solution.py
@@ -9,6 +9,11 @@
 HEAD_DIM = 128
 FF = 4096
 EXPERTS = 32
+
+
+def exchange_gather(x, mesh_axis, dim):
+    repeated = jnp.stack([x] * lax.axis_size(mesh_axis))
+    return jnp.concatenate(lax.all_to_all(repeated, mesh_axis, 0, 0), axis=dim)
 
 
 def attend(query, key_new, value_new, key_cache, value_cache, lengths):
@@ -69,7 +74,7 @@
     attended = attend(query, key_new, value_new, key_cache, value_cache, lengths)
     every_attended, every_hidden = (
         lax.all_gather(attended, "expert", axis=0, tiled=True),
-        lax.all_gather(hidden, "expert", axis=0, tiled=True),
+        exchange_gather(hidden, "expert", 0),
     )
     projected = jnp.dot(every_attended, w_out, preferred_element_type=jnp.float32).astype(
         jnp.bfloat16

time: 204 us -> 195 us (0.956)
  blocking collectives: 56.1 us -> 36.5 us
  starting transfers between devices: 0.01 us -> 6.33 us
    all_gather x1 -> x0, blocking collectives: 19.3 us -> none  [body(): lax.all_gather(hidden, 'expert', axis=0, tiled=True)]
    all_to_all x0 -> x1, starting transfers between devices: none -> 6.3 us  [exchange_gather(): return jnp.concatenate(lax.all_to_all(repeated, mesh_axis, 0, 0), axis=dim)]
  transfers between devices with their start and end apart: 1 -> 2, of which waited for: 1 -> 1; matrix products, arithmetic and copies ran while one was open for 0% -> 5% of each run, Pallas kernels for 0% -> 0%
where the time goes in v1:
time: 195 us; the launch traced here: 194 us
  waiting for transfers between devices  91.5 us (47%)
  blocking collectives  36.5 us (19%)
  matrix products  32 us (16%)
  between operations  14.2 us (7%)
  other arithmetic  8.67 us (4%)
  starting transfers between devices  6.33 us (3%)
  local copies, waits for them, and re-layouts  5.07 us (3%)
    unnamed x2, waiting for transfers between devices  91.5 us
    all_gather x1, blocking collectives, body(): lax.all_gather(attended, 'expert', axis=0, tiled=True)  18.9 us
    all_gather x1, blocking collectives, body(): every_projected = lax.all_gather(projected, 'expert', axis=1, tiled=True)  17.6 us
    dot_general x1, matrix products, body(): jnp.einsum('kcf,kfd->kcd', inner_act, down_local, preferred_element_type=...  12.8 us
    dot_general x1, matrix products, body(): jnp.einsum('kcd,dkf->kcf', picked, up_local, preferred_element_type=jnp.f...  12.2 us
    all_to_all x1, starting transfers between devices, exchange_gather(): return jnp.concatenate(lax.all_to_all(repeated, mesh_axis, 0, 0), axis=dim)  6.3 us
  transfers between devices with their start and end apart: 2, of which 1 were waited for; matrix products, arithmetic and copies ran while one was open for 5% of the time, Pallas kernels for 0%

profile of v1, /device:TPU:8, one launch (start us, length us, event | category | flops | bytes accessed | tf_op | source)
XLA Modules:
  0.0 194.3 jit_solution(66056128570978143)
XLA Ops:
  6.5 0.9 reduce.5
  7.5 0.5 broadcast.144
  8.0 1.0 reduce.9
  9.0 0.7 reshape.208
  9.7 6.3 %all-to-all-start = ((bf16[16,2,1024]{2,1,0:T(2,128)(2,1)}), bf16[16,2,1024]{2,1,0:T(2,128)(2,1)S(1)}, u32[]{:S(2)}, u32[]{:S(2)}) async-start(bf16[16,2,1024]{2,1,0:T(2,128)(2,1)} %reshape.208), calls=%async_computation | async-start | bytes 131072 | tf_op jit(solution)/shard_map/all_to_all | solution.py:16
  16.0 1.5 copy.43
  17.5 0.7 reduce.6
  18.2 0.9 fusion.42
  19.8 0.7 reduce.7
  21.1 1.5 copy.47
  22.6 0.7 convert_element_type.91
  23.7 18.9 %all-gather = bf16[16,1,2048]{2,1,0:T(2,128)(2,1)S(1)} all-gather(bf16[1,1,2048]{2,1,0:T(2,128)(2,1)S(1)} %reshape.192), channel_id=1, replica_groups=mesh['group'=2,'expert'=16] {'expert'}, dimensions={0}, use_global_device_ids=true | all-gather | bytes 69632 | tf_op jit(solution)/shard_map/all_gather | solution.py:76
  42.6 0.7 fusion.56
  43.5 1.2 convolution_convert_fusion.1
  44.8 0.7 convert_element_type.83
  45.5 17.6 %all_gather.7 = bf16[16,2048]{1,0:T(8,128)(2,1)S(1)} all-gather(bf16[16,128]{1,0:T(8,128)(2,1)S(1)} %convolution_convert_fusion.1), channel_id=1, replica_groups=mesh['group'=2,'expert'=16] {'expert'}, dimensions={1}, use_global_device_ids=true | all-gather | bytes 69632 | tf_op jit(solution)/shard_map/all_gather | solution.py:82
  63.6 1.2 fusion.3
  64.8 12.2 %fusion.15 = bf16[2,2,4096]{2,1,0:T(2,128)(2,1)S(1)} fusion(bf16[256,2,8,4096]{3,2,1,0:T(8,128)(2,1)} %bitcast.62, bf16[16,2048]{1,0:T(8,128)(2,1)S(1)} %multiply_convert_fusion, pred[16,2,2]{0,1,2:T(4,128)(4,1)S(1)} %compare_and_fusion), kind=kOutput, calls=%fused_computation.22 | convolution fusion | flops 67526656 | bytes 33652800 | tf_op jit(solution)/shard_map/kcd,dkf->kcf/dot_general | solution.py:113
  77.0 12.8 %fusion.60 = f32[2,2,2048]{2,1,0:T(2,128)S(1)} fusion(bf16[2,2,4096]{2,1,0:T(2,128)(2,1)S(1)} %fusion.15, bf16[2,4096,2048]{2,1,0:T(8,128)(2,1)} %bitcast.63), kind=kOutput, calls=%fused_computation.80 | convolution fusion | flops 67108864 | bytes 33619968 | tf_op jit(solution)/shard_map/kcf,kfd->kcd/dot_general | solution.py:117
  89.8 0.4 convolution_bitcast_fusion
  90.2 3.0 %convolution_add_fusion = f32[16,2048]{1,0:T(8,128)} fusion(f32[16,2048]{1,0:T(8,128)S(1)} %convolution_bitcast_fusion, bf16[512,2048]{1,0:T(8,128)(2,1)S(1)} %copy-done, bf16[16,2048]{1,0:T(8,128)(2,1)S(1)} %multiply_convert_fusion, bf16[2048,512]{1,0:T(8,128)(2,1)} %param.26), kind=kOutput, calls=%fused_computation.4 | convolution fusion | flops 67215360 | bytes 4521984 | tf_op jit(solution)/shard_map/dot_general | solution.py:120
  93.3 0.6 dynamic-slice
  93.9 91.4 %all-reduce.3.cloned.1.call-done = f32[16,2048]{1,0:T(8,128)} async-done(((f32[16,2048]{1,0:T(8,128)}), f32[16,2048]{1,0:T(8,128)}) %all-reduce.3.cloned.1.call-update) | async-done | bytes 131088
  185.4 2.1 %fusion.40 = bf16[1,2048]{1,0:T(2,128)(2,1)} fusion(f32[16,2048]{1,0:T(8,128)} %all-reduce.3.cloned.1.call-done, u32[]{:T(128)} %bitcast.13, f32[16,2048]{1,0:T(8,128)S(1)} %get-tuple-element.6, s32[]{:T(128)S(6)} %select_n.18), kind=kLoop, calls=%fused_computation.48 | loop fusion | flops 4096 | bytes 20488 | tf_op jit(solution)/shard_map/convert_element_type | solution.py:128
  (31 shorter events, 1.8 us)
Async XLA Ops:
  6.5 83.7 %copy-start = (bf16[512,2048]{1,0:T(8,128)(2,1)S(1)}, bf16[512,2048]{1,0:T(8,128)(2,1)}, u32[]{:S(2)}) copy-start(bf16[512,2048]{1,0:T(8,128)(2,1)} %param.27) | copy-start | bytes 6291460
  9.7 53.4 %all-to-all-start = ((bf16[16,2,1024]{2,1,0:T(2,128)(2,1)}), bf16[16,2,1024]{2,1,0:T(2,128)(2,1)S(1)}, u32[]{:S(2)}, u32[]{:S(2)}) async-start(bf16[16,2,1024]{2,1,0:T(2,128)(2,1)} %reshape.208), calls=%async_computation | async-start | bytes 131072 | tf_op jit(solution)/shard_map/all_to_all | solution.py:16
  16.0 169.4 %all-reduce.3.cloned.1.call-start = ((), (), s32[]{:S(2)}) async-start(), calls=%async_computation.1 | async-start | bytes 262144
  77.0 16.3 %copy-start.1 = (u32[32]{0:T(128)S(1)}, u32[32]{0:T(128)}, u32[]{:S(2)}) copy-start(u32[32]{0:T(128)} %constant.69) | copy-start | bytes 388
Sparse Core Ops, SparseCore 0:
  93.4 91.9 all-reduce.2
